TPU v7x, 32 devices: a whole 2x2x4 slice. The times are simulated.
32 devices in a mesh: tok: 8 (over z, y), voc: 4 (over x, core).
Axes of the slice: x: 2, y: 2, z: 4, core: 2. Of those that a mesh axis runs over, the one named last changes fastest.
Arguments:
- hidden: bfloat16 [96, 4096], P(('tok', 'voc'))
- head_weight: bfloat16 [4096, 16032], P(None, ('tok', 'voc'))
- actions: int32 [96], P(('tok', 'voc')), may hold values from 0 to 16031
- old_logp: bfloat16 [96], P(('tok', 'voc')), may hold values from -80 to 1
- advantage: bfloat16 [96], P(('tok', 'voc')), may hold values from -4 to 4
- loss_mask: int32 [96], P(('tok', 'voc')), may hold values 0 or 1
Outputs:
- grad_weight: bfloat16 [4096, 16032], P(None, ('tok', 'voc'))
- grad_hidden: float32 [96, 4096], P(('tok', 'voc'))
All inputs are finite; a program needn't handle non-finite values. No bound on the sum of `loss_mask` on one device may be relied on, other than what follows from the above.
Results may differ from a plain program's by a relative error of at most 0.0047.
Values may be sent and summed in bfloat16 or wider, within the bound.
A program may use at most 128 MiB of HBM per device.

v0:
```python
import jax
import jax.numpy as jnp
from jax import lax
from jax.sharding import PartitionSpec as P


def per_device(hidden, head_weight, actions, old_logp, advantage, loss_mask):
    hidden_all, old_all, advant_all = (
        lax.all_gather(hidden, ("tok", "voc"), axis=0, tiled=True),
        lax.all_gather(old_logp, ("tok", "voc"), axis=0, tiled=True),
        lax.all_gather(advantage, ("tok", "voc"), axis=0, tiled=True),
    )
    action_all, mask_all = (
        lax.all_gather(actions, ("tok", "voc"), axis=0, tiled=True),
        lax.all_gather(loss_mask, ("tok", "voc"), axis=0, tiled=True),
    )
    width = head_weight.shape[1]
    logits = jnp.dot(hidden_all, head_weight, preferred_element_type=jnp.float32)
    first_col = lax.axis_index(("tok", "voc")) * width
    columns = first_col + lax.broadcasted_iota(jnp.int32, logits.shape, 1)
    matches = columns == action_all[:, None]
    target_part = jnp.sum(jnp.where(matches, logits, 0.0), axis=1)
    top = lax.pmax(jnp.max(logits, axis=1), ("tok", "voc"))
    shifted = jnp.exp(logits - top[:, None])
    sumexp, moment, target = lax.psum(
        (jnp.sum(shifted, axis=1), jnp.sum(shifted * logits, axis=1), target_part), ("tok", "voc")
    )
    lse = top + jnp.log(sumexp)
    mean_logit = moment / sumexp
    advant = advant_all.astype(jnp.float32)
    ratio = jnp.exp(target - lse - old_all.astype(jnp.float32))
    clipped = (advant > 0.0) & (ratio > 1.2) | (advant < 0.0) & (ratio < 0.8)
    active = jnp.where(clipped, 0.0, 1.0).astype(jnp.float32)
    weights = mask_all.astype(jnp.float32)
    policy = -advant * ratio * active * weights
    probability = jnp.exp(logits - lse[:, None])
    onehot = matches.astype(jnp.float32)
    dlogits = policy[:, None] * (onehot - probability) + 0.05 * weights[:, None] * probability * (
        logits - mean_logit[:, None]
    )
    dlogits = dlogits.astype(jnp.bfloat16)
    partial_rows = lax.psum_scatter(
        lax.dot_general(
            dlogits, head_weight, (((1,), (1,)), ((), ())), preferred_element_type=jnp.float32
        ),
        "tok",
        scatter_dimension=0,
        tiled=True,
    )
    grad_hidden = lax.psum_scatter(partial_rows, "voc", scatter_dimension=0, tiled=True)
    grad_weight = lax.dot_general(
        hidden_all, dlogits, (((0,), (0,)), ((), ())), preferred_element_type=jnp.float32
    ).astype(jnp.bfloat16)
    return (grad_weight, grad_hidden)


def solution(mesh):
    placed = (
        P(("tok", "voc"), None),
        P(None, ("tok", "voc")),
        P(("tok", "voc")),
        P(("tok", "voc")),
        P(("tok", "voc")),
        P(("tok", "voc")),
    )
    return jax.shard_map(
        per_device,
        mesh=mesh,
        in_specs=placed,
        out_specs=(P(None, ("tok", "voc")), P(("tok", "voc"), None)),
        check_vma=False,
    )
```

profile of v0, /device:TPU:0, one launch (start us, length us, event | category | flops | bytes accessed | tf_op | source)
XLA Modules:
  0.0 323.1 jit_solution(7266715647205631639)
XLA Ops:
  7.2 0.0 copy-start.1
  7.2 0.0 all-reduce.12.cloned.1.call-start
  7.3 46.5 %all-gather = bf16[32,3,4096]{2,1,0:T(4,128)(2,1)S(1)} all-gather(bf16[1,3,4096]{2,1,0:T(4,128)(2,1)} %bitcast.11), channel_id=1, replica_groups=mesh['tok'=8,'voc'=4] {'tok','voc'}, dimensions={0}, use_global_device_ids=true | all-gather | bytes 811008 | tf_op jit(solution)/shard_map/all_gather | solution.py:9
  53.7 0.7 reshape.20
  54.4 3.6 %fusion.12 = (f32[96]{0:T(128)S(1)}, f32[96,501]{1,0:T(8,128)S(1)}) fusion(bf16[96,4096]{1,0:T(8,128)(2,1)S(1)} %reshape.20, bf16[4096,501]{0,1:T(8,128)(2,1)} %param.7), kind=kOutput, calls=%fused_computation.21 | convolution fusion | flops 394050432 | bytes 5083392 | tf_op jit(solution)/shard_map/dot_general | solution.py:18
  58.0 36.9 %pmax.7 = f32[96]{0:T(128)S(1)} all-reduce(f32[96]{0:T(128)S(1)} %get-tuple-element.16), channel_id=1, replica_groups=mesh['tok'=8,'voc'=4] {'tok','voc'}, use_global_device_ids=true, to_apply=%region_3.4 | all-reduce | flops 96 | bytes 768 | tf_op jit(solution)/shard_map/pmax | solution.py:23
  94.9 0.0 copy-done.1
  94.9 0.2 dynamic-update-slice.2
  95.1 0.0 copy-done.2
  95.1 0.2 dynamic-update-slice
  95.4 41.1 %all-reduce.9 = (bf16[96]{0:T(256)(128)(2,1)S(1)}, bf16[96]{0:T(256)(128)(2,1)S(1)}) all-reduce(bf16[96]{0:T(256)(128)(2,1)S(1)} %dynamic-update-slice.2, bf16[96]{0:T(256)(128)(2,1)S(1)} %dynamic-update-slice), channel_id=1, replica_groups=mesh['tok'=8,'voc'=4] {'tok','voc'}, use_global_device_ids=true, to_apply=%add.2 | all-reduce | flops 192 | bytes 768
  136.5 0.2 dynamic-update-slice.1
  136.7 0.2 dynamic-update-slice.3
  137.0 39.5 %all-reduce.7 = (s32[96]{0:T(128)S(1)}, s32[96]{0:T(128)S(1)}) all-reduce(s32[96]{0:T(128)S(1)} %dynamic-update-slice.1, s32[96]{0:T(128)S(1)} %dynamic-update-slice.3), channel_id=1, replica_groups=mesh['tok'=8,'voc'=4] {'tok','voc'}, use_global_device_ids=true, to_apply=%add.1 | all-reduce | flops 192 | bytes 1536
  176.4 0.2 fusion.7
  176.7 40.5 %all-reduce.8 = (f32[96]{0:T(128)S(1)}, f32[96]{0:T(128)S(1)}, f32[96]{0:T(128)S(1)}) all-reduce(f32[96]{0:T(128)S(1)} %get-tuple-element.3, f32[96]{0:T(128)S(1)} %get-tuple-element.2, f32[96]{0:T(128)S(1)} %get-tuple-element.4), channel_id=1, replica_groups=mesh['tok'=8,'voc'=4] {'tok','voc'}, use_global_device_ids=true, to_apply=%region_7.8 | all-reduce | flops 288 | bytes 2304 | tf_op jit(solution)/shard_map/psum | solution.py:25
  217.1 0.0 copy-start
  217.2 3.2 fusion.9
  220.3 46.1 %fusion = f32[16,4096]{1,0:T(8,128)S(1)} fusion(f32[96,4096]{1,0:T(8,128)S(1)} %fusion.9), kind=kCustom, calls=%all-reduce-scatter | all-reduce-scatter fusion | flops 524289 | bytes 1835520
  266.5 4.3 %collective-permute-start = (f32[16,4096]{1,0:T(8,128)S(1)}, f32[16,4096]{1,0:T(8,128)S(1)}, u32[]{:S(2)}, u32[]{:S(2)}) collective-permute-start(f32[16,4096]{1,0:T(8,128)S(1)} %fusion), channel_id=1, source_target_pairs={{0,4},{4,8},{8,12},{12,16},{16,20},{20,24},{24,28},{1,5},{5,9},{9,... | collective-permute-start | bytes 786440
  270.8 2.7 collective-permute-start.1
  273.5 0.6 dynamic-slice.6
  274.7 2.6 collective-permute-done.1
  277.3 0.0 collective-permute-done
  277.3 0.6 concatenate
  278.0 0.0 copy-start.5
  278.0 0.7 constant_dynamic-slice_fusion
  278.7 0.0 all-reduce.12.cloned.1.call-update
  278.7 3.4 %fusion.1 = bf16[4096,501]{0,1:T(8,128)(2,1)} fusion(bf16[96,4096]{1,0:T(8,128)(2,1)S(1)} %reshape.20, f32[96,501]{1,0:T(8,128)S(1)} %get-tuple-element.17, f32[96]{0:T(128)S(1)} %get-tuple-element.14, f32[96]{0:T(128)S(1)} %get-tuple-element.15, f32[96]{0:T(128)S(1)} %get-tuple-element.13, f32[96]{0:T(128)S(1)} %get-tuple-element.12, ...), kind=kOutput, calls=%fused_computation.1 | convolution fusion | flops 396535488 | bytes 5086932 | tf_op jit(solution)/shard_map/dot_general | solution.py:51
  282.1 0.6 dynamic-slice.2
  283.4 31.4 %all-reduce.12.cloned.1.call-done = f32[12,4096]{1,0:T(8,128)} async-done(((f32[12,4096]{1,0:T(8,128)}), f32[12,4096]{1,0:T(8,128)}) %all-reduce.12.cloned.1.call-update) | async-done | bytes 196624
  314.7 1.6 constant_dynamic-slice_fusion.1
  (14 shorter events, 0.1 us)
Async XLA Ops:
  7.2 87.7 %copy-start.1 = (bf16[3]{0:T(256)(128)(2,1)S(1)}, bf16[3]{0:T(256)(128)(2,1)}, u32[]{:S(2)}) copy-start(bf16[3]{0:T(256)(128)(2,1)} %param.9) | copy-start | bytes 22
  7.2 88.0 %copy-start.2 = (bf16[3]{0:T(256)(128)(2,1)S(1)}, bf16[3]{0:T(256)(128)(2,1)}, u32[]{:S(2)}) copy-start(bf16[3]{0:T(256)(128)(2,1)} %param.10) | copy-start | bytes 22
  7.2 129.3 %copy-start.3 = (s32[3]{0:T(128)S(1)}, s32[3]{0:T(128)}, u32[]{:S(2)}) copy-start(s32[3]{0:T(128)} %param.8) | copy-start | bytes 40
  7.2 129.5 %copy-start.4 = (s32[3]{0:T(128)S(1)}, s32[3]{0:T(128)}, u32[]{:S(2)}) copy-start(s32[3]{0:T(128)} %param.11) | copy-start | bytes 40
  7.2 307.5 %all-reduce.12.cloned.1.call-start = ((), (), s32[]{:S(2)}) async-start(), calls=%async_computation | async-start | bytes 524288
  217.1 56.3 %copy-start = (u32[32]{0:T(128)S(1)}, u32[32]{0:T(128)}, u32[]{:S(2)}) copy-start(u32[32]{0:T(128)} %constant.50) | copy-start | bytes 388
  266.5 10.9 %collective-permute-start = (f32[16,4096]{1,0:T(8,128)S(1)}, f32[16,4096]{1,0:T(8,128)S(1)}, u32[]{:S(2)}, u32[]{:S(2)}) collective-permute-start(f32[16,4096]{1,0:T(8,128)S(1)} %fusion), channel_id=1, source_target_pairs={{0,4},{4,8},{8,12},{12,16},{16,20},{20,24},{24,28},{1,5},{5,9},{9,... | collective-permute-start | bytes 786440
  270.8 6.6 %collective-permute-start.1 = (f32[12,4096]{1,0:T(8,128)S(1)}, f32[12,4096]{1,0:T(8,128)S(1)}, u32[]{:S(2)}, u32[]{:S(2)}) collective-permute-start(f32[12,4096]{1,0:T(8,128)S(1)} %slice), channel_id=1, source_target_pairs={{0,8},{4,12},{8,16},{12,20},{16,24},{20,28},{1,9},{5,13},{9,17},{1... | collective-permute-start | bytes 589832
  278.0 4.1 %copy-start.5 = (u32[32]{0:T(128)S(1)}, u32[32]{0:T(128)}, u32[]{:S(2)}) copy-start(u32[32]{0:T(128)} %constant.54) | copy-start | bytes 388
Sparse Core Ops, SparseCore 0:
  278.9 35.7 all-reduce.11
where the time goes:
time: 324 us; the launch traced here: 323 us
  blocking collectives  250 us (77%)
  waiting for transfers between devices  34 us (10%)
  between operations  15.5 us (5%)
  matrix products  10.2 us (3%)
  starting transfers between devices  7 us (2%)
  local copies, waits for them, and re-layouts  5.77 us (2%)
    unnamed x3, blocking collectives  127 us
    all_gather x1, blocking collectives, per_device(): lax.all_gather(hidden, ('tok', 'voc'), axis=0, tiled=True)  46.5 us
    psum x1, blocking collectives, per_device(): lax.psum((jnp.sum(shifted, axis=1), jnp.sum(shifted * logits, axis=1), ta...  40.5 us
    pmax x1, blocking collectives, per_device(): top = lax.pmax(jnp.max(logits, axis=1), ('tok', 'voc'))  36.9 us
    unnamed x4, waiting for transfers between devices  34 us
    unnamed x3, starting transfers between devices  7 us
  transfers between devices with their start and end apart: 3, of which 2 were waited for; matrix products, arithmetic and copies ran while one was open for 1% of the time, Pallas kernels for 0%

commit v1 on v0

--- a/solution.py
+++ b/solution.py
@@ -23,7 +23,8 @@
     top = lax.pmax(jnp.max(logits, axis=1), ("tok", "voc"))
     shifted = jnp.exp(logits - top[:, None])
     sumexp, moment, target = lax.psum(
-        (jnp.sum(shifted, axis=1), jnp.sum(shifted * logits, axis=1), target_part), ("tok", "voc")
+        lax.psum((jnp.sum(shifted, axis=1), jnp.sum(shifted * logits, axis=1), target_part), "tok"),
+        "voc",
     )
     lse = top + jnp.log(sumexp)
     mean_logit = moment / sumexp

time: 324 us -> 308 us (0.951)
  blocking collectives: 250 us -> 234 us
    psum x1, blocking collectives: 40.5 us -> 20.4 us  [per_device(): lax.psum((jnp.sum(shifted, axis=1), jnp.sum(shifted * logits, axis=1), ta...]
    psum x0 -> x1, blocking collectives: none -> 5.84 us  [per_device(): lax.psum(lax.psum((jnp.sum(shifted, axis=1), jnp.sum(shifted * logits, ax...]
where the time goes in v1:
time: 308 us; the launch traced here: 307 us
  blocking collectives  234 us (76%)
  waiting for transfers between devices  36.5 us (12%)
  between operations  15.5 us (5%)
  matrix products  10.2 us (3%)
  local copies, waits for them, and re-layouts  5.76 us (2%)
  starting transfers between devices  4.78 us (2%)
    unnamed x3, blocking collectives  125 us
    all_gather x1, blocking collectives, per_device(): lax.all_gather(hidden, ('tok', 'voc'), axis=0, tiled=True)  46.5 us
    pmax x1, blocking collectives, per_device(): top = lax.pmax(jnp.max(logits, axis=1), ('tok', 'voc'))  36.8 us
    unnamed x4, waiting for transfers between devices  36.5 us
    psum x1, blocking collectives, per_device(): lax.psum((jnp.sum(shifted, axis=1), jnp.sum(shifted * logits, axis=1), ta...  20.4 us
  transfers between devices with their start and end apart: 3, of which 2 were waited for; matrix products, arithmetic and copies ran while one was open for 1% of the time, Pallas kernels for 0%

profile of v1, /device:TPU:0, one launch (start us, length us, event | category | flops | bytes accessed | tf_op | source)
XLA Modules:
  0.0 307.4 jit_solution(1751652609228850190)
XLA Ops:
  7.2 0.0 copy-start.1
  7.2 0.0 copy-start.2
  7.2 0.0 all-reduce.13.cloned.1.call-start
  7.3 46.5 %all-gather = bf16[32,3,4096]{2,1,0:T(4,128)(2,1)S(1)} all-gather(bf16[1,3,4096]{2,1,0:T(4,128)(2,1)} %bitcast.11), channel_id=1, replica_groups=mesh['tok'=8,'voc'=4] {'tok','voc'}, dimensions={0}, use_global_device_ids=true | all-gather | bytes 811008 | tf_op jit(solution)/shard_map/all_gather | solution.py:9
  53.7 0.7 reshape.20
  54.4 3.6 %fusion.12 = (f32[96]{0:T(128)S(1)}, f32[96,501]{1,0:T(8,128)S(1)}) fusion(bf16[96,4096]{1,0:T(8,128)(2,1)S(1)} %reshape.20, bf16[4096,501]{0,1:T(8,128)(2,1)} %param.7), kind=kOutput, calls=%fused_computation.21 | convolution fusion | flops 394050432 | bytes 5083392 | tf_op jit(solution)/shard_map/dot_general | solution.py:18
  58.0 36.8 %pmax.7 = f32[96]{0:T(128)S(1)} all-reduce(f32[96]{0:T(128)S(1)} %get-tuple-element.19), channel_id=1, replica_groups=mesh['tok'=8,'voc'=4] {'tok','voc'}, use_global_device_ids=true, to_apply=%region_4.5 | all-reduce | flops 96 | bytes 768 | tf_op jit(solution)/shard_map/pmax | solution.py:23
  94.9 0.2 dynamic-update-slice.2
  95.1 0.2 dynamic-update-slice
  95.3 41.1 %all-reduce.10 = (bf16[96]{0:T(256)(128)(2,1)S(1)}, bf16[96]{0:T(256)(128)(2,1)S(1)}) all-reduce(bf16[96]{0:T(256)(128)(2,1)S(1)} %dynamic-update-slice.2, bf16[96]{0:T(256)(128)(2,1)S(1)} %dynamic-update-slice), channel_id=1, replica_groups=mesh['tok'=8,'voc'=4] {'tok','voc'}, use_global_device_ids=true, to_apply=%add.2 | all-reduce | flops 192 | bytes 768
  136.5 0.2 dynamic-update-slice.1
  136.7 0.2 dynamic-update-slice.3
  136.9 39.5 %all-reduce.7 = (s32[96]{0:T(128)S(1)}, s32[96]{0:T(128)S(1)}) all-reduce(s32[96]{0:T(128)S(1)} %dynamic-update-slice.1, s32[96]{0:T(128)S(1)} %dynamic-update-slice.3), channel_id=1, replica_groups=mesh['tok'=8,'voc'=4] {'tok','voc'}, use_global_device_ids=true, to_apply=%add.1 | all-reduce | flops 192 | bytes 1536
  176.4 0.2 fusion.7
  176.6 20.4 %all-reduce.8 = (f32[96]{0:T(128)S(1)}, f32[96]{0:T(128)S(1)}, f32[96]{0:T(128)S(1)}) all-reduce(f32[96]{0:T(128)S(1)} %get-tuple-element.3, f32[96]{0:T(128)S(1)} %get-tuple-element.2, f32[96]{0:T(128)S(1)} %get-tuple-element.4), channel_id=1, replica_groups=mesh['tok'=8,'voc'=4] {'tok'}, use_global_device_ids=true, to_apply=%region_9.10 | all-reduce | flops 288 | bytes 2304 | tf_op jit(solution)/shard_map/psum | solution.py:26
  197.0 5.8 %all-reduce.9 = (f32[96]{0:T(128)S(1)}, f32[96]{0:T(128)S(1)}, f32[96]{0:T(128)S(1)}) all-reduce(f32[96]{0:T(128)S(1)} %get-tuple-element.7, f32[96]{0:T(128)S(1)} %get-tuple-element.8, f32[96]{0:T(128)S(1)} %get-tuple-element.9), channel_id=1, replica_groups=mesh['tok'=8,'voc'=4] {'voc'}, use_global_device_ids=true, to_apply=%region_10.11 | all-reduce | flops 288 | bytes 2304 | tf_op jit(solution)/shard_map/psum | solution.py:25
  202.8 0.0 copy-start
  202.9 3.2 %fusion.9 = f32[96,4096]{1,0:T(8,128)S(1)} fusion(bf16[4096,501]{0,1:T(8,128)(2,1)} %param.7, f32[96,501]{1,0:T(8,128)S(1)} %get-tuple-element.20, f32[96]{0:T(128)S(1)} %get-tuple-element.17, f32[96]{0:T(128)S(1)} %get-tuple-element.18, f32[96]{0:T(128)S(1)} %get-tuple-element.16, f32[96]{0:T(128)S(1)} %get-tuple-element.15, s32[501]{0:T(512)S(1)} %iota_add_fusion, ...), kind=kOutput, calls=%fused_computation.20 | convolution fusion | flops 394483392 | bytes 5873364 | tf_op jit(solution)/shard_map/dot_general | solution.py:44
  206.0 44.3 %fusion = f32[16,4096]{1,0:T(8,128)S(1)} fusion(f32[96,4096]{1,0:T(8,128)S(1)} %fusion.9), kind=kCustom, calls=%all-reduce-scatter | all-reduce-scatter fusion | flops 524289 | bytes 1835520
  250.3 3.4 %collective-permute-start = (f32[16,4096]{1,0:T(8,128)S(1)}, f32[16,4096]{1,0:T(8,128)S(1)}, u32[]{:S(2)}, u32[]{:S(2)}) collective-permute-start(f32[16,4096]{1,0:T(8,128)S(1)} %fusion), channel_id=1, source_target_pairs={{0,4},{4,8},{8,12},{12,16},{16,20},{20,24},{24,28},{1,5},{5,9},{9,... | collective-permute-start | bytes 786440
  253.8 1.3 collective-permute-start.1
  255.1 0.6 dynamic-slice.6
  256.4 2.9 collective-permute-done.1
  259.3 0.0 collective-permute-done
  259.3 0.6 concatenate
  259.9 0.0 copy-start.5
  259.9 0.7 constant_dynamic-slice_fusion
  260.6 0.0 all-reduce.13.cloned.1.call-update
  260.7 3.4 %fusion.1 = bf16[4096,501]{0,1:T(8,128)(2,1)} fusion(bf16[96,4096]{1,0:T(8,128)(2,1)S(1)} %reshape.20, f32[96,501]{1,0:T(8,128)S(1)} %get-tuple-element.20, f32[96]{0:T(128)S(1)} %get-tuple-element.17, f32[96]{0:T(128)S(1)} %get-tuple-element.18, f32[96]{0:T(128)S(1)} %get-tuple-element.16, f32[96]{0:T(128)S(1)} %get-tuple-element.15, ...), kind=kOutput, calls=%fused_computation.1 | convolution fusion | flops 396535488 | bytes 5086932 | tf_op jit(solution)/shard_map/dot_general | solution.py:52
  264.0 0.6 dynamic-slice.2
  265.3 33.6 %all-reduce.13.cloned.1.call-done = f32[12,4096]{1,0:T(8,128)} async-done(((f32[12,4096]{1,0:T(8,128)}), f32[12,4096]{1,0:T(8,128)}) %all-reduce.13.cloned.1.call-update) | async-done | bytes 196624
  298.9 1.6 constant_dynamic-slice_fusion.1
  (15 shorter events, 0.1 us)
Async XLA Ops:
  7.2 87.7 %copy-start.1 = (bf16[3]{0:T(256)(128)(2,1)S(1)}, bf16[3]{0:T(256)(128)(2,1)}, u32[]{:S(2)}) copy-start(bf16[3]{0:T(256)(128)(2,1)} %param.9) | copy-start | bytes 22
  7.2 87.9 %copy-start.2 = (bf16[3]{0:T(256)(128)(2,1)S(1)}, bf16[3]{0:T(256)(128)(2,1)}, u32[]{:S(2)}) copy-start(bf16[3]{0:T(256)(128)(2,1)} %param.10) | copy-start | bytes 22
  7.2 129.3 %copy-start.3 = (s32[3]{0:T(128)S(1)}, s32[3]{0:T(128)}, u32[]{:S(2)}) copy-start(s32[3]{0:T(128)} %param.8) | copy-start | bytes 40
  7.2 129.5 %copy-start.4 = (s32[3]{0:T(128)S(1)}, s32[3]{0:T(128)}, u32[]{:S(2)}) copy-start(s32[3]{0:T(128)} %param.11) | copy-start | bytes 40
  7.2 291.7 %all-reduce.13.cloned.1.call-start = ((), (), s32[]{:S(2)}) async-start(), calls=%async_computation | async-start | bytes 524288
  202.8 52.3 %copy-start = (u32[32]{0:T(128)S(1)}, u32[32]{0:T(128)}, u32[]{:S(2)}) copy-start(u32[32]{0:T(128)} %constant.50) | copy-start | bytes 388
  250.3 8.9 %collective-permute-start = (f32[16,4096]{1,0:T(8,128)S(1)}, f32[16,4096]{1,0:T(8,128)S(1)}, u32[]{:S(2)}, u32[]{:S(2)}) collective-permute-start(f32[16,4096]{1,0:T(8,128)S(1)} %fusion), channel_id=1, source_target_pairs={{0,4},{4,8},{8,12},{12,16},{16,20},{20,24},{24,28},{1,5},{5,9},{9,... | collective-permute-start | bytes 786440
  253.8 5.5 %collective-permute-start.1 = (f32[12,4096]{1,0:T(8,128)S(1)}, f32[12,4096]{1,0:T(8,128)S(1)}, u32[]{:S(2)}, u32[]{:S(2)}) collective-permute-start(f32[12,4096]{1,0:T(8,128)S(1)} %slice), channel_id=1, source_target_pairs={{0,8},{4,12},{8,16},{12,20},{16,24},{20,28},{1,9},{5,13},{9,17},{1... | collective-permute-start | bytes 589832
  259.9 4.1 %copy-start.5 = (u32[32]{0:T(128)S(1)}, u32[32]{0:T(128)}, u32[]{:S(2)}) copy-start(u32[32]{0:T(128)} %constant.54) | copy-start | bytes 388
Sparse Core Ops, SparseCore 0:
  260.8 38.0 all-reduce.12
